TPU v7x, 256 devices: a whole 4x4x8 slice. The times are simulated.
256 devices in a mesh: gz: 16 (over z, y_lo), pa: 16 (over y_hi, x, core).
Axes of the slice: x: 4, y: 4 (y_hi: 2, y_lo: 2; y = y_hi * 2 + y_lo), z: 8, core: 2. Of those that a mesh axis runs over, the one named last changes fastest.
Arguments:
- density: bfloat16 [64, 1024, 1024], P('gz', 'pa'), may hold values from -6 to 6
- green: float32 [128, 1024, 1024], P('gz', 'pa'), may hold values from 0.1 to 3
Outputs:
- potential: float32 [64, 1024, 1024], P('gz', 'pa')
All inputs are finite; a program needn't handle non-finite values.
Results may differ from a plain program's by a relative error of at most 0.02.
Values may be sent and summed in bfloat16 or wider, within the bound.
A program may use at most 64 MiB of HBM per device.

v0:
```python
import math

import jax
import jax.numpy as jnp
import numpy as np
from jax import lax
from jax.sharding import PartitionSpec as P


def cas_table(rows, cols, length):
    product = np.arange(rows)[:, None] * np.arange(cols)[None, :] % length
    angle = product.astype(np.float32) * np.float32(2.0 * math.pi / length)
    return jnp.asarray((np.cos(angle) + np.sin(angle)).astype(np.float32), jnp.bfloat16)


def dot(spec, a, b):
    return jnp.einsum(spec, a, b, preferred_element_type=jnp.float32)


def exchange(value, axis):
    return lax.all_to_all(value, axis, split_axis=0, concat_axis=0, tiled=True)


def local(density, green, cas, cas_z):
    z_slab, x_local, y_cells = density.shape
    k_block, y_local, x_cells = green.shape
    groups = lax.axis_size("gz")
    pencils = lax.axis_size("pa")
    z_freqs = k_block * groups
    z_cells = z_slab * groups
    u_local = x_cells // groups
    half = jnp.bfloat16

    moved_green = green.astype(half).reshape(k_block, y_local, groups, u_local)
    moved_green = moved_green.transpose(2, 0, 1, 3).reshape(groups * k_block, y_local * u_local)
    moved_green = exchange(moved_green, "gz")

    yspec = dot("zxy,vy->vzx", density, cas).astype(half)
    yspec = exchange(yspec.reshape(y_cells, z_slab * x_local), "pa")
    yspec = yspec.reshape(pencils, y_local, z_slab, x_local)
    spectrum = dot("qvzl,uql->zvu", yspec, cas.reshape(x_cells, pencils, x_local)).astype(half)
    spectrum = spectrum.reshape(z_slab, y_local, groups, u_local).transpose(2, 0, 1, 3)
    spectrum = exchange(spectrum.reshape(groups * z_slab, y_local * u_local), "gz")
    spectrum = dot("kz,zs->ks", cas_z, spectrum)
    weighted = (moved_green.astype(jnp.float32) * spectrum).astype(half)
    back = dot("kz,ks->zs", cas_z, weighted).astype(half)
    back = exchange(back, "gz").reshape(groups, z_slab, y_local, u_local)
    back = dot("gzvu,xgu->xzv", back, cas.reshape(x_cells, groups, u_local)).astype(half)
    back = exchange(back.reshape(x_cells, z_slab * y_local), "pa")
    back = back.reshape(pencils, x_local, z_slab, y_local)
    total = dot("qlzv,yqv->zly", back, cas.reshape(y_cells, pencils, y_local))
    return total * (1.0 / (x_cells * y_cells * z_freqs))


def solution(mesh):
    cas = cas_table(1024, 1024, 1024)
    cas_z = cas_table(128, 64, 128)
    step = jax.shard_map(
        local,
        mesh=mesh,
        in_specs=(P("gz", "pa", None), P("gz", "pa", None), P(), P()),
        out_specs=P("gz", "pa", None),
        check_vma=False,
    )
    return lambda density, green: step(density, green, cas, cas_z)
```

profile of v0, /device:TPU:1, one launch (start us, length us, event | category | flops | bytes accessed | tf_op | source)
XLA Modules:
  0.0 133.4 jit_solution(14525277448841937380)
XLA Ops:
  0.0 0.0 copy-start
  0.0 1.0 copy-done
  1.0 2.3 %convolution_convert_fusion.1 = bf16[1024,4,64]{0,2,1:T(8,128)(2,1)S(1)} fusion(bf16[1024,1024,1]{1,0,2:T(8,128)(2,1)} %constant.11, bf16[4,64,1024]{2,1,0:T(8,128)(2,1)S(1)} %copy-done), kind=kOutput, calls=%fused_computation.10 | convolution fusion | flops 537133056 | bytes 3145728 | tf_op jit(solution)/shard_map/zxy,vy->vzx/dot_general | solution.py:17
  3.4 0.7 all_to_all.34
  4.0 0.8 copy.22
  4.9 19.2 %all_to_all.48 = bf16[16,64,256]{2,1,0:T(8,128)(2,1)S(1)} all-to-all(bf16[16,64,256]{2,1,0:T(8,128)(2,1)S(1)} %copy.22), channel_id=1, replica_groups=mesh['gz'=16,'pa'=16] {'pa'}, dimensions={0} | all-to-all | bytes 1048576 | tf_op jit(solution)/shard_map/all_to_all | solution.py:21
  24.1 0.4 reshape.44
  24.5 2.4 %fusion.7 = bf16[4,64,1024]{2,1,0:T(8,128)(2,1)S(1)} fusion(bf16[1024,16,64,1]{0,2,1,3:T(8,128)(2,1)} %constant.12, bf16[16,64,4,64]{3,2,1,0:T(4,128)(2,1)S(1)} %reshape.44), kind=kOutput, calls=%fused_computation.14 | convolution fusion | flops 537133056 | bytes 3145728 | tf_op jit(solution)/shard_map/qvzl,uql->zvu/dot_general | solution.py:17
  26.9 0.7 reshape.46
  27.5 0.3 copy.39
  27.8 0.8 all_to_all.36
  28.6 1.2 copy.25
  29.8 8.4 %all-to-all-start.2 = ((bf16[16,4,4096]{2,1,0:T(4,128)(2,1)}), bf16[16,4,4096]{2,1,0:T(4,128)(2,1)S(1)}, u32[]{:S(2)}, u32[]{:S(2)}) async-start(bf16[16,4,4096]{2,1,0:T(4,128)(2,1)} %copy.25), calls=%async_computation.2 | async-start | bytes 1048576 | tf_op jit(solution)/shard_map/all_to_all | solution.py:21
  38.2 2.7 %convert_element_type.33 = bf16[8,64,1024]{2,1,0:T(8,128)(2,1)} convert(f32[8,64,1024]{2,1,0:T(8,128)} %param.5) | non-fusion elementwise | flops 524288 | bytes 3145728 | tf_op jit(solution)/shard_map/convert_element_type | solution.py:34
  41.0 2.9 %reshape.43 = bf16[8,64,16,64]{3,2,1,0:T(8,128)(2,1)S(1)} reshape(bf16[8,64,1024]{2,1,0:T(8,128)(2,1)} %convert_element_type.33) | data formatting | bytes 2097152 | tf_op jit(solution)/shard_map/reshape | solution.py:34
  43.9 1.9 %copy.38 = bf16[8,64,16,64]{3,1,0,2:T(8,128)(2,1)} copy(bf16[8,64,16,64]{3,2,1,0:T(8,128)(2,1)S(1)} %reshape.43) | data formatting | bytes 2097152 | tf_op jit(solution)/shard_map/reshape | solution.py:34
  45.8 4.1 %all_to_all.32 = bf16[16,8,4096]{2,1,0:T(8,128)(2,1)} reshape(bf16[16,8,64,64]{3,2,1,0:T(8,128)(2,1)} %bitcast.64) | data formatting | bytes 2097152 | tf_op jit(solution)/shard_map/all_to_all | solution.py:21
  50.0 3.5 %all-to-all-done.2 = bf16[16,4,4096]{2,1,0:T(4,128)(2,1)S(1)} async-done(((bf16[16,4,4096]{2,1,0:T(4,128)(2,1)}), bf16[16,4,4096]{2,1,0:T(4,128)(2,1)S(1)}, u32[]{:S(2)}, u32[]{:S(2)}) %all-to-all-start.2) | async-done | bytes 524320 | tf_op jit(solution)/shard_map/all_to_all | solution.py:21
  53.5 4.2 %all-to-all-start = ((bf16[16,8,4096]{2,1,0:T(8,128)(2,1)}), bf16[16,8,4096]{2,1,0:T(8,128)(2,1)S(1)}, u32[]{:S(2)}, u32[]{:S(2)}) async-start(bf16[16,8,4096]{2,1,0:T(8,128)(2,1)} %all_to_all.32), calls=%async_computation | async-start | bytes 2097152 | tf_op jit(solution)/shard_map/all_to_all | solution.py:21
  57.7 0.1 all_to_all.38
  57.8 24.3 %all-to-all-done = bf16[16,8,4096]{2,1,0:T(8,128)(2,1)S(1)} async-done(((bf16[16,8,4096]{2,1,0:T(8,128)(2,1)}), bf16[16,8,4096]{2,1,0:T(8,128)(2,1)S(1)}, u32[]{:S(2)}, u32[]{:S(2)}) %all-to-all-start) | async-done | bytes 1048608 | tf_op jit(solution)/shard_map/all_to_all | solution.py:21
  82.2 0.6 fusion.1
  82.7 0.2 all_to_all.39
  82.9 22.8 %all_to_all.49 = bf16[16,4,4096]{2,1,0:T(4,128)(2,1)S(1)} all-to-all(bf16[16,4,4096]{2,1,0:T(4,128)(2,1)S(1)} %all_to_all.39), channel_id=1, replica_groups=mesh['gz'=16,'pa'=16] {'gz'}, dimensions={0} | all-to-all | bytes 1048576 | tf_op jit(solution)/shard_map/all_to_all | solution.py:21
  105.8 0.3 copy.26
  106.1 1.1 reshape.47
  107.2 2.4 %fusion.6 = bf16[1024,4,64]{0,2,1:T(8,128)(2,1)S(1)} fusion(bf16[16,4,64,64]{3,2,0,1:T(8,128)(2,1)S(1)} %reshape.47, bf16[1024,16,64,1]{0,2,1,3:T(8,128)(2,1)} %constant.12), kind=kOutput, calls=%fused_computation.13 | convolution fusion | flops 537133056 | bytes 3145728 | tf_op jit(solution)/shard_map/gzvu,xgu->xzv/dot_general | solution.py:17
  109.6 0.7 all_to_all.41
  110.2 0.8 copy.27
  111.1 18.6 %all_to_all.50 = bf16[16,64,256]{2,1,0:T(8,128)(2,1)S(1)} all-to-all(bf16[16,64,256]{2,1,0:T(8,128)(2,1)S(1)} %copy.27), channel_id=1, replica_groups=mesh['gz'=16,'pa'=16] {'pa'}, dimensions={0} | all-to-all | bytes 1048576 | tf_op jit(solution)/shard_map/all_to_all | solution.py:21
  129.7 0.4 reshape.48
  130.1 3.3 %fusion.3 = f32[4,64,1024]{2,1,0:T(8,128)} fusion(bf16[1024,16,64,1]{0,2,1,3:T(8,128)(2,1)} %constant.12, bf16[16,64,4,64]{3,2,1,0:T(4,128)(2,1)S(1)} %reshape.48), kind=kOutput, calls=%fused_computation.7 | convolution fusion | flops 537133056 | bytes 3670016 | tf_op jit(solution)/shard_map/qlzv,yqv->zly/dot_general | solution.py:17
  (2 shorter events, 0.0 us)
Async XLA Ops:
  0.0 1.0 copy-start
  29.8 23.6 %all-to-all-start.2 = ((bf16[16,4,4096]{2,1,0:T(4,128)(2,1)}), bf16[16,4,4096]{2,1,0:T(4,128)(2,1)S(1)}, u32[]{:S(2)}, u32[]{:S(2)}) async-start(bf16[16,4,4096]{2,1,0:T(4,128)(2,1)} %copy.25), calls=%async_computation.2 | async-start | bytes 1048576 | tf_op jit(solution)/shard_map/all_to_all | solution.py:21
  50.0 32.2 %copy-start.1 = (bf16[128,64]{1,0:T(8,128)(2,1)S(1)}, bf16[128,64]{1,0:T(8,128)(2,1)}, u32[]{:S(2)}) copy-start(bf16[128,64]{1,0:T(8,128)(2,1)} %constant.7.clone) | copy-start | bytes 49156
  53.5 28.7 %all-to-all-start = ((bf16[16,8,4096]{2,1,0:T(8,128)(2,1)}), bf16[16,8,4096]{2,1,0:T(8,128)(2,1)S(1)}, u32[]{:S(2)}, u32[]{:S(2)}) async-start(bf16[16,8,4096]{2,1,0:T(8,128)(2,1)} %all_to_all.32), calls=%async_computation | async-start | bytes 2097152 | tf_op jit(solution)/shard_map/all_to_all | solution.py:21
where the time goes:
time: 134 us; the launch traced here: 133 us
  blocking collectives  60.7 us (45%)
  waiting for transfers between devices  27.8 us (21%)
  local copies, waits for them, and re-layouts  18.5 us (14%)
  starting transfers between devices  12.6 us (9%)
  matrix products  10.9 us (8%)
  other arithmetic  2.73 us (2%)
    all_to_all x3, blocking collectives, exchange(): return lax.all_to_all(value, axis, split_axis=0, concat_axis=0, tiled=True)  60.7 us
    all_to_all x2, waiting for transfers between devices, exchange(): return lax.all_to_all(value, axis, split_axis=0, concat_axis=0, tiled=True)  27.8 us
    all_to_all x2, starting transfers between devices, exchange(): return lax.all_to_all(value, axis, split_axis=0, concat_axis=0, tiled=True)  12.6 us
    dot_general x5, matrix products, dot(): return jnp.einsum(spec, a, b, preferred_element_type=jnp.float32)  10.9 us
    all_to_all x10, local copies, waits for them, and re-layouts, exchange(): return lax.all_to_all(value, axis, split_axis=0, concat_axis=0, tiled=True)  9.75 us
    reshape x2, local copies, waits for them, and re-layouts, local(): moved_green = green.astype(half).reshape(k_block, y_local, groups, u_local)  4.85 us
    convert_element_type x1, other arithmetic, local(): moved_green = green.astype(half).reshape(k_block, y_local, groups, u_local)  2.73 us
  transfers between devices with their start and end apart: 2, of which 2 were waited for; matrix products, arithmetic and copies ran while one was open for 6% of the time, Pallas kernels for 0%

commit v1 on v0

v1 whole, which is shorter than its diff:
```python
import math

import jax
import jax.numpy as jnp
import numpy as np
from jax import lax
from jax.experimental import pallas as pl
from jax.experimental.pallas import tpu as pltpu
from jax.sharding import PartitionSpec as P

MESH = pl.DeviceIdType.MESH
HALF = jnp.bfloat16
N = 16


def cas_table(rows, cols, length):
    product = np.arange(rows)[:, None] * np.arange(cols)[None, :] % length
    angle = product.astype(np.float32) * np.float32(2.0 * math.pi / length)
    return jnp.asarray((np.cos(angle) + np.sin(angle)).astype(np.float32), HALF)


def dot(a, b):
    return jnp.dot(a, b, preferred_element_type=jnp.float32)


def dot_nt(a, b):
    return lax.dot_general(a, b, (((1,), (1,)), ((), ())), preferred_element_type=jnp.float32)


def iota(shape, dim):
    return lax.broadcasted_iota(jnp.int32, shape, dim)


def block(index, size):
    return pl.ds(pl.multiple_of(index * size, size), size)


def kernel(
    scale,
    density_hbm,
    green_hbm,
    cas_hbm,
    casz_ref,
    caszt_ref,
    out_ref,
    rhs,
    green_in,
    cas,
    cas2,
    kron_f,
    kron_i,
    green_out,
    green_all,
    y_out,
    y_all,
    lhs,
    x_out,
    x_all,
    z_in,
    z_mid,
    z_out,
    z_all,
    i_out,
    i_all,
    load_sem,
    send_sem,
    recv_sem,
):
    me_g = lax.axis_index("gz")
    me_p = lax.axis_index("pa")
    me = {"gz": me_g, "pa": me_p}

    loads = [
        pltpu.make_async_copy(source, target, load_sem.at[i])
        for i, (source, target) in enumerate(
            ((cas_hbm, cas), (density_hbm, rhs), (green_hbm, green_in))
        )
    ]
    for load in loads:
        load.start()

    barrier = pltpu.get_barrier_semaphore()
    for axis in ("gz", "pa"):

        @pl.loop(1, N)
        def _(s, axis=axis):
            pl.semaphore_signal(
                barrier, inc=1, device_id={axis: lax.rem(me[axis] + s, N)}, device_id_type=MESH
            )

    def copy(which, axis, source, target, peer):
        s = lax.rem(peer - me[axis] + N, N)
        return pltpu.make_async_remote_copy(
            src_ref=source.at[peer],
            dst_ref=target.at[me[axis]],
            send_sem=send_sem.at[which, s],
            recv_sem=recv_sem.at[which, s],
            device_id={axis: peer},
            device_id_type=MESH,
        )

    def send(which, axis, source, target, peer):
        @pl.when(peer != me[axis])
        def _():
            copy(which, axis, source, target, peer).start()

        @pl.when(peer == me[axis])
        def _():
            target[me[axis]] = source[me[axis]]

    def send_all(which, axis, source, target):
        @pl.loop(0, N)
        def _(i):
            far = jnp.where(lax.rem(i, 2) == 0, N // 2 + i // 2, N // 2 - (i + 1) // 2)
            send(which, axis, source, target, lax.rem(me[axis] + far, N))

    def receive(which, axis, source, target):
        @pl.loop(1, N)
        def _(s):
            copy(which, axis, source, target, lax.rem(me[axis] + s, N)).wait_recv()

    def drain(which, axis, source, target):
        @pl.loop(1, N)
        def _(s):
            copy(which, axis, source, target, lax.rem(me[axis] + s, N)).wait_send()

    loads[0].wait()
    loads[1].wait()

    @pl.loop(0, 4)
    def _(j):
        value = dot_nt(cas[block(j, 256), :], rhs[...]).astype(HALF)
        for i in range(4):
            y_out[4 * j + i] = value[64 * i : 64 * (i + 1), :]

    loads[2].wait()

    @pl.loop(0, 8)
    def _(k):
        for b in range(8):
            value = green_in[k, :, 128 * b : 128 * (b + 1)].astype(HALF)
            green_out[2 * b, k] = value[:32]
            green_out[2 * b + 1, k] = value[32:]

    pl.semaphore_wait(barrier, 2 * (N - 1))
    send_all(0, "pa", y_out, y_all)
    send_all(1, "gz", green_out, green_all)

    @pl.loop(0, N)
    def _(q):
        value = cas[block(q, 64), :]
        cas2[block(2 * q, 64), :] = value
        cas2[block(2 * q + 1, 64), :] = value

    def spread(table, target, rows, cols):
        @pl.loop(0, rows // 16)
        def _(j):
            pick = (iota((128, rows), 0) >> 3) + 16 * j == iota((128, rows), 1)
            part = dot(pick.astype(jnp.float32).astype(HALF), table[...]).astype(HALF)
            wide = (iota((cols, 8 * cols), 1) >> 3) == iota((cols, 8 * cols), 0)
            full = dot(part, wide.astype(jnp.float32).astype(HALF))
            same = (iota((128, 8 * cols), 0) & 7) == (iota((128, 8 * cols), 1) & 7)
            target[block(j, 128), :] = jnp.where(same, full, 0.0).astype(HALF)

    spread(casz_ref, kron_f, 128, 64)
    spread(caszt_ref, kron_i, 64, 128)

    low = (iota((64, 128), 1) < 64).astype(jnp.float32).astype(HALF)
    masks = (low, (1.0 - low.astype(jnp.float32)).astype(HALF))

    def spread_planes(source):
        @pl.loop(0, N)
        def _(q):
            for z in range(4):
                part = source[q, :, 128 * (z // 2) : 128 * (z // 2 + 1)]
                lhs[64 * z : 64 * (z + 1), block(q, 128)] = part * masks[z % 2]

    receive(0, "pa", y_out, y_all)
    spread_planes(y_all)

    @pl.loop(0, 4)
    def _(i):
        j = lax.rem(i + me_g // 4 + 1, 4)
        value = dot(lhs[...], cas2[:, block(j, 256)]).astype(HALF)
        for u in range(2):
            for v in range(2):
                for z in range(4):
                    row = 64 * z + 32 * v
                    x_out[4 * j + 2 * u + v, z] = value[row : row + 32, 128 * u : 128 * (u + 1)]
        for b in range(4):
            send(2, "gz", x_out, x_all, 4 * j + b)

    receive(2, "gz", x_out, x_all)
    receive(1, "gz", green_out, green_all)

    for h in range(2):
        rows = slice(16 * h, 16 * h + 16)

        @pl.loop(0, N)
        def _(g):
            value = x_all[g, :, rows, :].astype(jnp.float32)
            for v in range(2):
                part = value[:, 8 * v : 8 * v + 8, :].reshape(32, 128)
                z_in[block(g, 32), 128 * v : 128 * (v + 1)] = part.astype(HALF)

        @pl.loop(0, 4)
        def _(j):
            value = dot(kron_f[block(j, 256), :], z_in[...])
            for i in range(4):
                weight = green_all[4 * j + i, :, rows, :].astype(jnp.float32)
                for v in range(2):
                    part = weight[:, 8 * v : 8 * v + 8, :].reshape(64, 128)
                    part = part * value[64 * i : 64 * i + 64, 128 * v : 128 * (v + 1)]
                    z_mid[pl.ds(pl.multiple_of(256 * j + 64 * i, 64), 64), 128 * v : 128 * (v + 1)] = part.astype(HALF)

        @pl.loop(0, 2)
        def _(j):
            value = dot(kron_i[block(j, 256), :], z_mid[...])
            for i in range(8):
                part = value[32 * i : 32 * i + 32]
                part = jnp.concatenate(
                    [part[:, 128 * v : 128 * (v + 1)].reshape(4, 8, 128) for v in range(2)], axis=1
                )
                z_out[8 * j + i, :, rows, :] = part.astype(HALF)

    send_all(3, "gz", z_out, z_all)
    receive(3, "gz", z_out, z_all)

    @pl.loop(0, 8)
    def _(u):
        for v in range(2):
            for z in range(4):
                row = 64 * z + 32 * v
                rhs[row : row + 32, block(u, 128)] = z_all[2 * u + v, z]

    @pl.loop(0, 4)
    def _(i):
        j = lax.rem(i + me_p // 4 + 1, 4)
        value = dot_nt(cas[block(j, 256), :], rhs[...]).astype(HALF)
        for b in range(4):
            i_out[4 * j + b] = value[64 * b : 64 * (b + 1), :]
            send(4, "pa", i_out, i_all, 4 * j + b)

    receive(4, "pa", i_out, i_all)
    spread_planes(i_all)

    @pl.loop(0, 4)
    def _(j):
        out_ref[:, block(j, 256)] = dot(lhs[...], cas2[:, block(j, 256)]) * scale

    drain(0, "pa", y_out, y_all)
    drain(1, "gz", green_out, green_all)
    drain(2, "gz", x_out, x_all)
    drain(3, "gz", z_out, z_all)
    drain(4, "pa", i_out, i_all)


def solution(mesh):
    cas = cas_table(1024, 1024, 1024)
    cas_z = cas_table(128, 64, 128)
    cas_zt = cas_table(64, 128, 128)
    scale = 1.0 / (1024 * 1024 * 128)

    def local(density, green, cas, cas_z, cas_zt):
        def vmem(*shape, dtype=HALF):
            return pltpu.VMEM(shape, dtype)

        anywhere = pl.BlockSpec(memory_space=pl.ANY)
        near = pl.BlockSpec(memory_space=pltpu.VMEM)
        potential = pl.pallas_call(
            lambda *refs: kernel(scale, *refs),
            out_shape=jax.ShapeDtypeStruct((256, 1024), jnp.float32),
            in_specs=[anywhere, anywhere, anywhere, near, near],
            out_specs=near,
            scratch_shapes=[
                vmem(256, 1024),
                vmem(8, 64, 1024, dtype=jnp.float32),
                vmem(1024, 1024),
                vmem(2048, 1024),
                vmem(1024, 512),
                vmem(512, 1024),
                vmem(N, 8, 32, 128),
                vmem(N, 8, 32, 128),
                vmem(N, 64, 256),
                vmem(N, 64, 256),
                vmem(256, 2048),
                vmem(N, 4, 32, 128),
                vmem(N, 4, 32, 128),
                vmem(512, 256),
                vmem(1024, 256),
                vmem(N, 4, 32, 128),
                vmem(N, 4, 32, 128),
                vmem(N, 64, 256),
                vmem(N, 64, 256),
                pltpu.SemaphoreType.DMA((3,)),
                pltpu.SemaphoreType.DMA((5, N)),
                pltpu.SemaphoreType.DMA((5, N)),
            ],
            compiler_params=pltpu.CompilerParams(
                collective_id=0, has_side_effects=True, vmem_limit_bytes=60 * 1024 * 1024
            ),
            name="poisson",
        )(density.reshape(256, 1024), green, cas, cas_z, cas_zt)
        return potential.reshape(4, 64, 1024)

    step = jax.shard_map(
        local,
        mesh=mesh,
        in_specs=(P("gz", "pa", None), P("gz", "pa", None), P(), P(), P()),
        out_specs=P("gz", "pa", None),
        check_vma=False,
    )
    return lambda density, green: step(density, green, cas, cas_z, cas_zt)
```

time: 134 us -> 81.8 us (0.61)
  Pallas kernels: 0 us -> 79.3 us
  blocking collectives: 60.7 us -> 0 us
  waiting for transfers between devices: 27.8 us -> 0 us
  local copies, waits for them, and re-layouts: 18.5 us -> 2.31 us
  starting transfers between devices: 12.6 us -> 0 us
  matrix products: 10.9 us -> 0 us
  other arithmetic: 2.73 us -> 0 us
    pallas_call x0 -> x1, Pallas kernels: none -> 79.3 us  [local(): pl.pallas_call(lambda *refs: kernel(scale, *refs), out_shape=jax.ShapeDty...]
    all_to_all x3 -> x0, blocking collectives: 60.7 us -> none  [exchange(): return lax.all_to_all(value, axis, split_axis=0, concat_axis=0, tiled=True)]
    all_to_all x2 -> x0, waiting for transfers between devices: 27.8 us -> none  [exchange(): return lax.all_to_all(value, axis, split_axis=0, concat_axis=0, tiled=True)]
    all_to_all x2 -> x0, starting transfers between devices: 12.6 us -> none  [exchange(): return lax.all_to_all(value, axis, split_axis=0, concat_axis=0, tiled=True)]
    dot_general x5 -> x0, matrix products: 10.9 us -> none  [dot(): return jnp.einsum(spec, a, b, preferred_element_type=jnp.float32)]
    all_to_all x10 -> x0, local copies, waits for them, and re-layouts: 9.75 us -> none  [exchange(): return lax.all_to_all(value, axis, split_axis=0, concat_axis=0, tiled=True)]
    reshape x7 -> x0, local copies, waits for them, and re-layouts: 7.71 us -> none  [the longest x2 4.85 us: local(): moved_green = green.astype(half).reshape(k_block, y_local, groups, u_local)]
    convert_element_type x1 -> x0, other arithmetic: 2.73 us -> none  [local(): moved_green = green.astype(half).reshape(k_block, y_local, groups, u_local)]
  transfers between devices with their start and end apart: 2 -> 0, of which waited for: 2 -> 0; matrix products, arithmetic and copies ran while one was open for 6% -> 0% of each run, Pallas kernels for 0% -> 0%
where the time goes in v1:
time: 81.8 us; the launch traced here: 81.6 us
  Pallas kernels  79.3 us (97%)
  local copies, waits for them, and re-layouts  2.31 us (3%)
    pallas_call x1, Pallas kernels, local(): pl.pallas_call(lambda *refs: kernel(scale, *refs), out_shape=jax.ShapeDty...  79.3 us
    unnamed x1, local copies, waits for them, and re-layouts  2.31 us

profile of v1, /device:TPU:1, one launch (start us, length us, event | category | flops | bytes accessed | tf_op | source)
XLA Modules:
  0.0 81.6 jit_solution(14026996768960145097)
XLA Ops:
  0.0 79.3 %poisson.1 = f32[256,1024]{1,0:T(8,128)} custom-call(bf16[256,1024]{1,0:T(8,128)(2,1)} %bitcast.3, f32[8,64,1024]{2,1,0:T(8,128)} %refs_1_.1, bf16[1024,1024]{1,0:T(8,128)(2,1)} %constant.6.clone.refs_2_, bf16[128,64]{1,0:T(8,128)(2,1)} %constant.7.clone.refs_3_, bf16[64,128]{1,0:T(8,128)(2,1)} %constant.8.clone.refs_4_), custom_call_target="tpu_custom_call" | custom-call | tf_op jit(solution)/shard_map/poisson/pallas_call | solution.py:270
  79.3 2.3 %copy.7 = f32[4,64,1024]{2,1,0:T(8,128)} copy(f32[4,64,1024]{2,1,0:T(8,128)} %bitcast.2) | data formatting | bytes 2097152

commit v2 on v1

v2 whole, which is shorter than its diff:
```python
import math

import jax
import jax.numpy as jnp
import numpy as np
from jax import lax
from jax.experimental import pallas as pl
from jax.experimental.pallas import tpu as pltpu
from jax.sharding import PartitionSpec as P

MESH = pl.DeviceIdType.MESH
HALF = jnp.bfloat16
N = 16
PARTS = 2


def cas_table(rows, cols, length):
    product = np.arange(rows)[:, None] * np.arange(cols)[None, :] % length
    angle = product.astype(np.float32) * np.float32(2.0 * math.pi / length)
    return jnp.asarray((np.cos(angle) + np.sin(angle)).astype(np.float32), HALF)


def dot(a, b):
    return jnp.dot(a, b, preferred_element_type=jnp.float32)


def dot_nt(a, b):
    return lax.dot_general(a, b, (((1,), (1,)), ((), ())), preferred_element_type=jnp.float32)


def iota(shape, dim):
    return lax.broadcasted_iota(jnp.int32, shape, dim)


def one_hot(condition):
    return condition.astype(jnp.float32).astype(HALF)


def block(index, size):
    return pl.ds(pl.multiple_of(index * size, size), size)


def kernel(
    scale,
    density_hbm,
    green_hbm,
    cas_hbm,
    casz_ref,
    caszt_ref,
    out_ref,
    planes,
    green_in,
    cas,
    cas2,
    cas4,
    kron_f,
    kron_i,
    green_out,
    green_all,
    y_out,
    y_all,
    lhs_x,
    x_out,
    x_all,
    z_in,
    z_mid,
    z_out,
    z_all,
    rhs,
    i_out,
    i_all,
    lhs_y,
    load_sem,
    send_sem,
    recv_sem,
):
    me = {"gz": lax.axis_index("gz"), "pa": lax.axis_index("pa")}

    loads = [
        pltpu.make_async_copy(source, target, load_sem.at[i])
        for i, (source, target) in enumerate(
            ((cas_hbm, cas), (density_hbm, planes), (green_hbm, green_in))
        )
    ]
    for load in loads:
        load.start()

    barrier = pltpu.get_barrier_semaphore()
    for axis in ("gz", "pa"):

        @pl.loop(1, N)
        def _(s, axis=axis):
            pl.semaphore_signal(
                barrier, inc=1, device_id={axis: lax.rem(me[axis] + s, N)}, device_id_type=MESH
            )

    class Exchange:
        def __init__(self, number, axis, source, target):
            self.number, self.axis, self.source, self.target = number, axis, source, target

        def copy(self, peer):
            mine = me[self.axis]
            s = lax.rem(peer - mine + N, N)
            return pltpu.make_async_remote_copy(
                src_ref=self.source.at[peer],
                dst_ref=self.target.at[mine],
                send_sem=send_sem.at[self.number, s],
                recv_sem=recv_sem.at[self.number, s],
                device_id={self.axis: peer},
                device_id_type=MESH,
            )

        def send(self, peer):
            mine = me[self.axis]

            @pl.when(peer != mine)
            def _():
                self.copy(peer).start()

            @pl.when(peer == mine)
            def _():
                self.target[mine] = self.source[mine]

        def send_all(self):
            @pl.loop(0, N)
            def _(i):
                far = jnp.where(lax.rem(i, 2) == 0, N // 2 + i // 2, N // 2 - (i + 1) // 2)
                self.send(lax.rem(me[self.axis] + far, N))

        def receive(self):
            @pl.loop(1, N)
            def _(s):
                self.copy(lax.rem(me[self.axis] + s, N)).wait_recv()

        def drain(self):
            @pl.loop(1, N)
            def _(s):
                self.copy(lax.rem(me[self.axis] + s, N)).wait_send()

    ex_y = Exchange(0, "pa", y_out, y_all)
    ex_green = [Exchange(1 + h, "gz", green_out.at[h], green_all.at[h]) for h in range(PARTS)]
    ex_x = [Exchange(3 + h, "gz", x_out.at[h], x_all.at[h]) for h in range(PARTS)]
    ex_z = [Exchange(5 + h, "gz", z_out.at[h], z_all.at[h]) for h in range(PARTS)]
    ex_i = [Exchange(7 + h, "pa", i_out.at[h], i_all.at[h]) for h in range(PARTS)]

    def y_forward():
        @pl.loop(0, 4)
        def _(j):
            value = dot_nt(cas[block(j, 256), :], planes[...]).astype(HALF)
            for i in range(4):
                y_out[4 * j + i] = value[64 * i : 64 * (i + 1), :]

    def green_narrow():
        @pl.loop(0, 8)
        def _(k):
            for u in range(8):
                value = green_in[k, :, 128 * u : 128 * (u + 1)].astype(HALF)
                for v in range(2):
                    for h in range(PARTS):
                        row = 32 * v + 16 * h
                        green_out[h, 2 * u + v, k] = value[row : row + 16]

    def tables():
        @pl.loop(0, N)
        def _(q):
            value = cas[block(q, 64), :]
            cas2[block(2 * q, 64), :] = value
            cas2[block(2 * q + 1, 64), :] = value
            for h in range(PARTS):
                for z in range(4):
                    for v in range(2):
                        row = 32 * v + 16 * h
                        cas4[h, block(q * 8 + z * 2 + v, 16), :] = value[row : row + 16]

        def spread(table, target, rows, cols):
            @pl.loop(0, rows // 16)
            def _(j):
                pick = (iota((128, rows), 0) >> 3) + 16 * j == iota((128, rows), 1)
                part = dot(one_hot(pick), table[...]).astype(HALF)
                wide = (iota((cols, 8 * cols), 1) >> 3) == iota((cols, 8 * cols), 0)
                full = dot(part, one_hot(wide))
                same = (iota((128, 8 * cols), 0) & 7) == (iota((128, 8 * cols), 1) & 7)
                target[block(j, 128), :] = jnp.where(same, full, 0.0).astype(HALF)

        spread(casz_ref, kron_f, 128, 64)
        spread(caszt_ref, kron_i, 64, 128)

    lane = iota((64, 128), 1)

    def x_operand():
        masks = [one_hot((lane >> 6) == z) for z in range(2)]

        @pl.loop(0, N)
        def _(q):
            for z in range(4):
                part = y_all[q, :, 128 * (z // 2) : 128 * (z // 2 + 1)] * masks[z % 2]
                for h in range(PARTS):
                    for v in range(2):
                        row = 32 * v + 16 * h
                        to = 128 * h + 32 * z + 16 * v
                        lhs_x[to : to + 16, block(q, 128)] = part[row : row + 16]

    def x_forward(h):
        @pl.loop(0, 4)
        def _(i):
            j = lax.rem(i + me["gz"] // 4 + 1, 4)
            value = dot(lhs_x[128 * h : 128 * (h + 1), :], cas2[:, block(j, 256)]).astype(HALF)
            for u in range(2):
                for v in range(2):
                    for z in range(4):
                        row = 32 * z + 16 * v
                        x_out[h, 4 * j + 2 * u + v, z] = value[
                            row : row + 16, 128 * u : 128 * (u + 1)
                        ]
            for b in range(4):
                ex_x[h].send(4 * j + b)

    def z_both(h):
        @pl.loop(0, N)
        def _(g):
            value = x_all[h, g].astype(jnp.float32)
            for v in range(2):
                part = value[:, 8 * v : 8 * v + 8, :].reshape(32, 128)
                z_in[block(g, 32), 128 * v : 128 * (v + 1)] = part.astype(HALF)

        @pl.loop(0, 4)
        def _(j):
            value = dot(kron_f[block(j, 256), :], z_in[...])
            for i in range(4):
                weight = green_all[h, 4 * j + i].astype(jnp.float32)
                for v in range(2):
                    part = weight[:, 8 * v : 8 * v + 8, :].reshape(64, 128)
                    part = part * value[64 * i : 64 * i + 64, 128 * v : 128 * (v + 1)]
                    z_mid[block(4 * j + i, 64), 128 * v : 128 * (v + 1)] = part.astype(HALF)

        @pl.loop(0, 2)
        def _(i):
            j = lax.rem(i + me["gz"] // 8 + 1, 2)
            value = dot(kron_i[block(j, 256), :], z_mid[...])
            for b in range(8):
                part = value[32 * b : 32 * b + 32]
                part = jnp.concatenate(
                    [part[:, 128 * v : 128 * (v + 1)].reshape(4, 8, 128) for v in range(2)], axis=1
                )
                z_out[h, 8 * j + b] = part.astype(HALF)
            for b in range(8):
                ex_z[h].send(8 * j + b)

    def x_inverse(h):
        @pl.loop(0, 8)
        def _(u):
            for v in range(2):
                for z in range(4):
                    row = 32 * z + 16 * v
                    rhs[row : row + 16, block(u, 128)] = z_all[h, 2 * u + v, z]

        @pl.loop(0, 4)
        def _(i):
            j = lax.rem(i + me["pa"] // 4 + 1, 4)
            value = dot_nt(cas[block(j, 256), :], rhs[...]).astype(HALF)
            for b in range(4):
                i_out[h, 4 * j + b] = value[64 * b : 64 * (b + 1), :]
            for b in range(4):
                ex_i[h].send(4 * j + b)

    def y_inverse(h):
        masks = [one_hot((lane >> 5) == z) for z in range(4)]

        @pl.loop(0, N)
        def _(q):
            value = i_all[h, q]
            for z in range(4):
                lhs_y[64 * z : 64 * (z + 1), block(q, 128)] = value * masks[z]

        @pl.loop(0, 4)
        def _(j):
            value = dot(lhs_y[...], cas4[h, :, block(j, 256)])
            if h == 0:
                out_ref[:, block(j, 256)] = value
            else:
                out_ref[:, block(j, 256)] = (out_ref[:, block(j, 256)] + value) * scale

    scope = jax.named_scope
    with scope("load"):
        loads[0].wait()
        loads[1].wait()
    with scope("y_forward"):
        y_forward()
    with scope("green_narrow"):
        loads[2].wait()
        green_narrow()
    with scope("barrier"):
        pl.semaphore_wait(barrier, 2 * (N - 1))
    with scope("send_y"):
        ex_y.send_all()
        ex_green[0].send_all()
    with scope("tables"):
        tables()
    with scope("wait_y"):
        ex_y.receive()
    with scope("x_operand"):
        x_operand()
    with scope("x_forward0"):
        x_forward(0)
    with scope("send_green1"):
        ex_green[1].send_all()
    with scope("x_forward1"):
        x_forward(1)
    for h in range(PARTS):
        with scope(f"wait_green{h}"):
            ex_green[h].receive()
        with scope(f"wait_x{h}"):
            ex_x[h].receive()
        with scope(f"z_both{h}"):
            z_both(h)
    for h in range(PARTS):
        with scope(f"wait_z{h}"):
            ex_z[h].receive()
        with scope(f"x_inverse{h}"):
            x_inverse(h)
    for h in range(PARTS):
        with scope(f"wait_i{h}"):
            ex_i[h].receive()
        with scope(f"y_inverse{h}"):
            y_inverse(h)
    with scope("drain"):
        for exchange in [ex_y, *ex_green, *ex_x, *ex_z, *ex_i]:
            exchange.drain()


def solution(mesh):
    cas = cas_table(1024, 1024, 1024)
    cas_z = cas_table(128, 64, 128)
    cas_zt = cas_table(64, 128, 128)
    scale = 1.0 / (1024 * 1024 * 128)

    def local(density, green, cas, cas_z, cas_zt):
        def vmem(*shape, dtype=HALF):
            return pltpu.VMEM(shape, dtype)

        anywhere = pl.BlockSpec(memory_space=pl.ANY)
        near = pl.BlockSpec(memory_space=pltpu.VMEM)
        potential = pl.pallas_call(
            lambda *refs: kernel(scale, *refs),
            out_shape=jax.ShapeDtypeStruct((256, 1024), jnp.float32),
            in_specs=[anywhere, anywhere, anywhere, near, near],
            out_specs=near,
            scratch_shapes=[
                vmem(256, 1024),
                vmem(8, 64, 1024, dtype=jnp.float32),
                vmem(1024, 1024),
                vmem(2048, 1024),
                vmem(PARTS, 2048, 1024),
                vmem(1024, 512),
                vmem(512, 1024),
                vmem(PARTS, N, 8, 16, 128),
                vmem(PARTS, N, 8, 16, 128),
                vmem(N, 64, 256),
                vmem(N, 64, 256),
                vmem(256, 2048),
                vmem(PARTS, N, 4, 16, 128),
                vmem(PARTS, N, 4, 16, 128),
                vmem(512, 256),
                vmem(1024, 256),
                vmem(PARTS, N, 4, 16, 128),
                vmem(PARTS, N, 4, 16, 128),
                vmem(128, 1024),
                vmem(PARTS, N, 64, 128),
                vmem(PARTS, N, 64, 128),
                vmem(256, 2048),
                pltpu.SemaphoreType.DMA((3,)),
                pltpu.SemaphoreType.DMA((9, N)),
                pltpu.SemaphoreType.DMA((9, N)),
            ],
            compiler_params=pltpu.CompilerParams(
                collective_id=0, has_side_effects=True, vmem_limit_bytes=60 * 1024 * 1024
            ),
            name="poisson",
        )(density.reshape(256, 1024), green, cas, cas_z, cas_zt)
        return potential.reshape(4, 64, 1024)

    step = jax.shard_map(
        local,
        mesh=mesh,
        in_specs=(P("gz", "pa", None), P("gz", "pa", None), P(), P(), P()),
        out_specs=P("gz", "pa", None),
        check_vma=False,
    )
    return lambda density, green: step(density, green, cas, cas_z, cas_zt)
```

time: 81.8 us -> 75.1 us (0.918)
  Pallas kernels: 79.3 us -> 72.6 us
    pallas_call x1, Pallas kernels: 79.3 us -> 72.6 us  [local(): pl.pallas_call(lambda *refs: kernel(scale, *refs), out_shape=jax.ShapeDty...]
where the time goes in v2:
time: 75.1 us; the launch traced here: 74.9 us
  Pallas kernels  72.6 us (97%)
  local copies, waits for them, and re-layouts  2.31 us (3%)
    pallas_call x1, Pallas kernels, local(): pl.pallas_call(lambda *refs: kernel(scale, *refs), out_shape=jax.ShapeDty...  72.6 us
    unnamed x1, local copies, waits for them, and re-layouts  2.31 us

profile of v2, /device:TPU:1, one launch (start us, length us, event | category | flops | bytes accessed | tf_op | source)
XLA Modules:
  0.0 74.9 jit_solution(887939767744506866)
XLA Ops:
  0.0 72.6 %poisson.1 = f32[256,1024]{1,0:T(8,128)} custom-call(bf16[256,1024]{1,0:T(8,128)(2,1)} %bitcast.3, f32[8,64,1024]{2,1,0:T(8,128)} %refs_1_.1, bf16[1024,1024]{1,0:T(8,128)(2,1)} %constant.6.clone.refs_2_, bf16[128,64]{1,0:T(8,128)(2,1)} %constant.7.clone.refs_3_, bf16[64,128]{1,0:T(8,128)(2,1)} %constant.8.clone.refs_4_), custom_call_target="tpu_custom_call" | custom-call | tf_op jit(solution)/shard_map/poisson/pallas_call | solution.py:343
  72.6 2.3 %copy.7 = f32[4,64,1024]{2,1,0:T(8,128)} copy(f32[4,64,1024]{2,1,0:T(8,128)} %bitcast.2) | data formatting | bytes 2097152

commit v3 on v2

--- a/solution.py
+++ b/solution.py
@@ -12,6 +12,7 @@
 HALF = jnp.bfloat16
 N = 16
 PARTS = 2
+FAR_FIRST = [8, 7, 9, 6, 10, 5, 11, 4, 12, 3, 13, 2, 14, 1, 15]
 
 
 def cas_table(rows, cols, length):
@@ -41,12 +42,9 @@
 
 
 def kernel(
-    scale,
     density_hbm,
     green_hbm,
     cas_hbm,
-    casz_ref,
-    caszt_ref,
     out_ref,
     planes,
     green_in,
@@ -70,6 +68,7 @@
     i_out,
     i_all,
     lhs_y,
+    part_i,
     load_sem,
     send_sem,
     recv_sem,
@@ -79,17 +78,15 @@
     loads = [
         pltpu.make_async_copy(source, target, load_sem.at[i])
         for i, (source, target) in enumerate(
-            ((cas_hbm, cas), (density_hbm, planes), (green_hbm, green_in))
+            ((green_hbm, green_in), (cas_hbm, cas), (density_hbm, planes))
         )
     ]
     for load in loads:
         load.start()
 
     barrier = pltpu.get_barrier_semaphore()
-    for axis in ("gz", "pa"):
-
-        @pl.loop(1, N)
-        def _(s, axis=axis):
+    for s in FAR_FIRST:
+        for axis in ("gz", "pa"):
             pl.semaphore_signal(
                 barrier, inc=1, device_id={axis: lax.rem(me[axis] + s, N)}, device_id_type=MESH
             )
@@ -110,31 +107,45 @@
                 device_id_type=MESH,
             )
 
-        def send(self, peer):
+        def arrive(self, peer):
+            s = lax.rem(me[self.axis] - peer + N, N)
+            pltpu.make_async_remote_copy(
+                src_ref=self.source.at[peer],
+                dst_ref=self.target.at[peer],
+                send_sem=send_sem.at[self.number, s],
+                recv_sem=recv_sem.at[self.number, s],
+                device_id={self.axis: peer},
+                device_id_type=MESH,
+            ).wait_recv()
+
+        def keep(self):
             mine = me[self.axis]
-
-            @pl.when(peer != mine)
-            def _():
-                self.copy(peer).start()
-
-            @pl.when(peer == mine)
-            def _():
-                self.target[mine] = self.source[mine]
-
-        def send_all(self):
-            @pl.loop(0, N)
-            def _(i):
-                far = jnp.where(lax.rem(i, 2) == 0, N // 2 + i // 2, N // 2 - (i + 1) // 2)
-                self.send(lax.rem(me[self.axis] + far, N))
-
-        def receive(self):
-            @pl.loop(1, N)
-            def _(s):
-                self.copy(lax.rem(me[self.axis] + s, N)).wait_recv()
+            self.target[mine] = self.source[mine]
+
+        def send(self, steps=FAR_FIRST):
+            for s in steps:
+                self.copy(lax.rem(me[self.axis] + s, N)).start()
+
+        def peer(self, turn, b):
+            mine = me[self.axis]
+            return 4 * lax.rem(mine // 4 + turn, 4) + lax.rem(lax.rem(mine, 4) + b, 4)
+
+        def send_group(self, turn, own):
+            if own:
+                self.keep()
+            for b in range(1 if own else 0, 4):
+                self.copy(self.peer(turn, b)).start()
+
+        def receive(self, steps=FAR_FIRST):
+            for s in steps:
+                self.arrive(lax.rem(me[self.axis] + s, N))
+
+        def receive_group(self, turn):
+            for b in range(0 if turn else 1, 4):
+                self.arrive(self.peer(turn, b))
 
         def drain(self):
-            @pl.loop(1, N)
-            def _(s):
+            for s in FAR_FIRST:
                 self.copy(lax.rem(me[self.axis] + s, N)).wait_send()
 
     ex_y = Exchange(0, "pa", y_out, y_all)
@@ -172,18 +183,18 @@
                         row = 32 * v + 16 * h
                         cas4[h, block(q * 8 + z * 2 + v, 16), :] = value[row : row + 16]
 
-        def spread(table, target, rows, cols):
+        def spread(target, rows, cols):
             @pl.loop(0, rows // 16)
             def _(j):
-                pick = (iota((128, rows), 0) >> 3) + 16 * j == iota((128, rows), 1)
-                part = dot(one_hot(pick), table[...]).astype(HALF)
-                wide = (iota((cols, 8 * cols), 1) >> 3) == iota((cols, 8 * cols), 0)
+                pick = 8 * ((iota((128, 1024), 0) >> 3) + 16 * j) == iota((128, 1024), 1)
+                part = dot(one_hot(pick), cas[:, :128]).astype(HALF)
+                wide = (iota((128, 8 * cols), 1) >> 3) == iota((128, 8 * cols), 0)
                 full = dot(part, one_hot(wide))
                 same = (iota((128, 8 * cols), 0) & 7) == (iota((128, 8 * cols), 1) & 7)
                 target[block(j, 128), :] = jnp.where(same, full, 0.0).astype(HALF)
 
-        spread(casz_ref, kron_f, 128, 64)
-        spread(caszt_ref, kron_i, 64, 128)
+        spread(kron_f, 128, 64)
+        spread(kron_i, 64, 128)
 
     lane = iota((64, 128), 1)
 
@@ -201,9 +212,8 @@
                         lhs_x[to : to + 16, block(q, 128)] = part[row : row + 16]
 
     def x_forward(h):
-        @pl.loop(0, 4)
-        def _(i):
-            j = lax.rem(i + me["gz"] // 4 + 1, 4)
+        def group(turn, own):
+            j = lax.rem(me["gz"] // 4 + turn, 4)
             value = dot(lhs_x[128 * h : 128 * (h + 1), :], cas2[:, block(j, 256)]).astype(HALF)
             for u in range(2):
                 for v in range(2):
@@ -212,8 +222,13 @@
                         x_out[h, 4 * j + 2 * u + v, z] = value[
                             row : row + 16, 128 * u : 128 * (u + 1)
                         ]
-            for b in range(4):
-                ex_x[h].send(4 * j + b)
+            ex_x[h].send_group(turn, own)
+
+        @pl.loop(1, 4)
+        def _(turn):
+            group(turn, False)
+
+        group(0, True)
 
     def z_both(h):
         @pl.loop(0, N)
@@ -234,8 +249,7 @@
                     z_mid[block(4 * j + i, 64), 128 * v : 128 * (v + 1)] = part.astype(HALF)
 
         @pl.loop(0, 2)
-        def _(i):
-            j = lax.rem(i + me["gz"] // 8 + 1, 2)
+        def _(j):
             value = dot(kron_i[block(j, 256), :], z_mid[...])
             for b in range(8):
                 part = value[32 * b : 32 * b + 32]
@@ -243,58 +257,81 @@
                     [part[:, 128 * v : 128 * (v + 1)].reshape(4, 8, 128) for v in range(2)], axis=1
                 )
                 z_out[h, 8 * j + b] = part.astype(HALF)
-            for b in range(8):
-                ex_z[h].send(8 * j + b)
+
+        ex_z[h].send()
+        ex_z[h].keep()
 
     def x_inverse(h):
-        @pl.loop(0, 8)
-        def _(u):
-            for v in range(2):
-                for z in range(4):
-                    row = 32 * z + 16 * v
-                    rhs[row : row + 16, block(u, 128)] = z_all[h, 2 * u + v, z]
-
-        @pl.loop(0, 4)
-        def _(i):
-            j = lax.rem(i + me["pa"] // 4 + 1, 4)
-            value = dot_nt(cas[block(j, 256), :], rhs[...]).astype(HALF)
-            for b in range(4):
-                i_out[h, 4 * j + b] = value[64 * b : 64 * (b + 1), :]
-            for b in range(4):
-                ex_i[h].send(4 * j + b)
-
-    def y_inverse(h):
-        masks = [one_hot((lane >> 5) == z) for z in range(4)]
-
-        @pl.loop(0, N)
-        def _(q):
-            value = i_all[h, q]
-            for z in range(4):
-                lhs_y[64 * z : 64 * (z + 1), block(q, 128)] = value * masks[z]
-
-        @pl.loop(0, 4)
-        def _(j):
-            value = dot(lhs_y[...], cas4[h, :, block(j, 256)])
-            if h == 0:
-                out_ref[:, block(j, 256)] = value
-            else:
-                out_ref[:, block(j, 256)] = (out_ref[:, block(j, 256)] + value) * scale
+        for last, turns in enumerate(((2, 1), (3, 0))):
+            for turn in turns:
+                ex_z[h].receive_group(turn)
+            groups = [lax.rem(me["gz"] // 4 + turn, 4) for turn in turns]
+            for t, j in enumerate(groups):
+                for u in range(2):
+                    for v in range(2):
+                        for z in range(4):
+                            row = 32 * z + 16 * v
+                            column = 256 * t + 128 * u
+                            rhs[last, row : row + 16, column : column + 128] = z_all[
+                                h, 4 * j + 2 * u + v, z
+                            ]
+            for to in (1, 2, 3, 0):
+                i = lax.rem(me["pa"] // 4 + to, 4)
+                value = sum(
+                    dot_nt(
+                        cas[block(i, 256), block(j, 256)], rhs[last, :, 256 * t : 256 * (t + 1)]
+                    )
+                    for t, j in enumerate(groups)
+                )
+                if last:
+                    value = (value + part_i[block(i, 256), :]).astype(HALF)
+                    for b in range(4):
+                        i_out[h, 4 * i + b] = value[64 * b : 64 * (b + 1), :]
+                    ex_i[h].send_group(to, to == 0)
+                else:
+                    part_i[block(i, 256), :] = value
+
+    masks = [one_hot((lane >> 5) == z) for z in range(4)]
+
+    def y_inverse(h, steps):
+        for step, turns in enumerate(steps):
+            for turn in turns:
+                ex_i[h].receive_group(turn)
+            groups = [lax.rem(me["pa"] // 4 + turn, 4) for turn in turns]
+            for i in groups:
+                for b in range(4):
+                    value = i_all[h, 4 * i + b]
+                    for z in range(4):
+                        lhs_y[64 * z : 64 * (z + 1), block(4 * i + b, 128)] = value * masks[z]
+            for j in range(4):
+                columns = slice(256 * j, 256 * (j + 1))
+                value = sum(
+                    dot(lhs_y[:, block(i, 512)], cas4[h, block(i, 512), columns]) for i in groups
+                )
+                if h or step:
+                    value = value + out_ref[:, columns]
+                out_ref[:, columns] = value
 
     scope = jax.named_scope
+    with scope("load_green"):
+        loads[0].wait()
+    with scope("green_narrow"):
+        green_narrow()
     with scope("load"):
-        loads[0].wait()
         loads[1].wait()
+        loads[2].wait()
     with scope("y_forward"):
         y_forward()
-    with scope("green_narrow"):
-        loads[2].wait()
-        green_narrow()
     with scope("barrier"):
         pl.semaphore_wait(barrier, 2 * (N - 1))
     with scope("send_y"):
-        ex_y.send_all()
-        ex_green[0].send_all()
+        ex_green[0].send()
+        ex_y.send()
+        ex_green[1].send(FAR_FIRST[:7])
     with scope("tables"):
+        ex_green[0].keep()
+        ex_green[1].keep()
+        ex_y.keep()
         tables()
     with scope("wait_y"):
         ex_y.receive()
@@ -303,47 +340,75 @@
     with scope("x_forward0"):
         x_forward(0)
     with scope("send_green1"):
-        ex_green[1].send_all()
+        ex_green[1].send(FAR_FIRST[7:])
     with scope("x_forward1"):
         x_forward(1)
-    for h in range(PARTS):
-        with scope(f"wait_green{h}"):
-            ex_green[h].receive()
-        with scope(f"wait_x{h}"):
-            ex_x[h].receive()
-        with scope(f"z_both{h}"):
-            z_both(h)
-    for h in range(PARTS):
-        with scope(f"wait_z{h}"):
-            ex_z[h].receive()
-        with scope(f"x_inverse{h}"):
-            x_inverse(h)
-    for h in range(PARTS):
-        with scope(f"wait_i{h}"):
-            ex_i[h].receive()
-        with scope(f"y_inverse{h}"):
-            y_inverse(h)
+    with scope("drain_early"):
+        ex_y.drain()
+        ex_green[0].drain()
+    with scope("wait_green0"):
+        ex_green[0].receive()
+    with scope("wait_x0"):
+        ex_x[0].receive()
+    with scope("z_both0"):
+        z_both(0)
+    with scope("wait_green1"):
+        ex_green[1].receive()
+    with scope("drain_x0"):
+        ex_x[0].drain()
+    with scope("wait_x1"):
+        ex_x[1].receive()
+    with scope("z_both1"):
+        z_both(1)
+    with scope("drain_x1"):
+        ex_green[1].drain()
+        ex_x[1].drain()
+    with scope("x_inverse0"):
+        x_inverse(0)
+    with scope("drain_z0"):
+        ex_z[0].drain()
+    with scope("x_inverse1"):
+        x_inverse(1)
+    with scope("y_inverse0"):
+        y_inverse(0, ((0, 1, 3, 2),))
+    with scope("drain_z1"):
+        ex_z[1].drain()
+        ex_i[0].drain()
+    with scope("y_inverse1"):
+        y_inverse(1, ((0, 1), (3,), (2,)))
     with scope("drain"):
-        for exchange in [ex_y, *ex_green, *ex_x, *ex_z, *ex_i]:
-            exchange.drain()
+        ex_i[1].drain()
+
+
+def finish(scale, total, out_hbm, held, sem):
+    rows = held.shape[0] // 4
+    writes = [
+        pltpu.make_async_copy(
+            held.at[pl.ds(rows * i, rows)], out_hbm.at[pl.ds(rows * i, rows)], sem.at[i]
+        )
+        for i in range(4)
+    ]
+    for i, write in enumerate(writes):
+        held[rows * i : rows * (i + 1), :] = total[rows * i : rows * (i + 1), :] * scale
+        write.start()
+    for write in writes:
+        write.wait()
 
 
 def solution(mesh):
     cas = cas_table(1024, 1024, 1024)
-    cas_z = cas_table(128, 64, 128)
-    cas_zt = cas_table(64, 128, 128)
     scale = 1.0 / (1024 * 1024 * 128)
 
-    def local(density, green, cas, cas_z, cas_zt):
+    def local(density, green, cas):
         def vmem(*shape, dtype=HALF):
             return pltpu.VMEM(shape, dtype)
 
         anywhere = pl.BlockSpec(memory_space=pl.ANY)
         near = pl.BlockSpec(memory_space=pltpu.VMEM)
         potential = pl.pallas_call(
-            lambda *refs: kernel(scale, *refs),
+            kernel,
             out_shape=jax.ShapeDtypeStruct((256, 1024), jnp.float32),
-            in_specs=[anywhere, anywhere, anywhere, near, near],
+            in_specs=[anywhere, anywhere, anywhere],
             out_specs=near,
             scratch_shapes=[
                 vmem(256, 1024),
@@ -364,26 +429,39 @@
                 vmem(1024, 256),
                 vmem(PARTS, N, 4, 16, 128),
                 vmem(PARTS, N, 4, 16, 128),
-                vmem(128, 1024),
+                vmem(2, 128, 512),
                 vmem(PARTS, N, 64, 128),
                 vmem(PARTS, N, 64, 128),
                 vmem(256, 2048),
+                vmem(1024, 128, dtype=jnp.float32),
                 pltpu.SemaphoreType.DMA((3,)),
                 pltpu.SemaphoreType.DMA((9, N)),
                 pltpu.SemaphoreType.DMA((9, N)),
             ],
             compiler_params=pltpu.CompilerParams(
-                collective_id=0, has_side_effects=True, vmem_limit_bytes=60 * 1024 * 1024
+                collective_id=0, has_side_effects=True, vmem_limit_bytes=48 * 1024 * 1024
             ),
             name="poisson",
-        )(density.reshape(256, 1024), green, cas, cas_z, cas_zt)
+        )(*[pltpu.with_memory_space_constraint(x, pltpu.HBM) for x in (density.reshape(256, 1024), green, cas)])
+        potential = pl.pallas_call(
+            lambda *refs: finish(scale, *refs),
+            out_shape=jax.ShapeDtypeStruct((256, 1024), jnp.float32),
+            in_specs=[near],
+            out_specs=anywhere,
+            scratch_shapes=[
+                vmem(256, 1024, dtype=jnp.float32),
+                pltpu.SemaphoreType.DMA((4,)),
+            ],
+            compiler_params=pltpu.CompilerParams(vmem_limit_bytes=8 * 1024 * 1024),
+            name="finish",
+        )(potential)
         return potential.reshape(4, 64, 1024)
 
     step = jax.shard_map(
         local,
         mesh=mesh,
-        in_specs=(P("gz", "pa", None), P("gz", "pa", None), P(), P(), P()),
+        in_specs=(P("gz", "pa", None), P("gz", "pa", None), P()),
         out_specs=P("gz", "pa", None),
         check_vma=False,
     )
-    return lambda density, green: step(density, green, cas, cas_z, cas_zt)
+    return lambda density, green: step(density, green, cas)

time: 75.1 us -> 69.5 us (0.925)
  Pallas kernels: 72.6 us -> 69.4 us
  local copies, waits for them, and re-layouts: 2.31 us -> 0 us
    pallas_call x1 -> x2, Pallas kernels: 72.6 us -> 69.4 us  [the longest x1 68.4 us: local(): pl.pallas_call(kernel, out_shape=jax.ShapeDtypeStruct((256, 1024), jnp.fl...]
    unnamed x1 -> x0, local copies, waits for them, and re-layouts: 2.31 us -> none
where the time goes in v3:
time: 69.5 us; the launch traced here: 69.4 us
  Pallas kernels  69.4 us (100%)
    pallas_call x1, Pallas kernels, local(): pl.pallas_call(kernel, out_shape=jax.ShapeDtypeStruct((256, 1024), jnp.fl...  68.4 us

profile of v3, /device:TPU:1, one launch (start us, length us, event | category | flops | bytes accessed | tf_op | source)
XLA Modules:
  0.0 69.4 jit_solution(1997924461314089198)
XLA Ops:
  0.0 68.4 %poisson.1.refs_0_ = f32[256,1024]{1,0:T(8,128)S(1)} custom-call(bf16[256,1024]{1,0:T(8,128)(2,1)} %bitcast.2, f32[8,64,1024]{2,1,0:T(8,128)} %green_hbm.1, bf16[1024,1024]{1,0:T(8,128)(2,1)} %constant.2.clone.cas_hbm), custom_call_target="tpu_custom_call" | custom-call | tf_op jit(solution)/shard_map/poisson/pallas_call | solution.py:408
  68.4 1.0 %finish.1 = f32[256,1024]{1,0:T(8,128)} custom-call(f32[256,1024]{1,0:T(8,128)S(1)} %poisson.1.refs_0_), custom_call_target="tpu_custom_call" | custom-call | tf_op jit(solution)/shard_map/finish/pallas_call | solution.py:446

commit v4 on v3

--- a/solution.py
+++ b/solution.py
@@ -42,6 +42,7 @@
 
 
 def kernel(
+    scale,
     density_hbm,
     green_hbm,
     cas_hbm,
@@ -91,6 +92,9 @@
                 barrier, inc=1, device_id={axis: lax.rem(me[axis] + s, N)}, device_id_type=MESH
             )
 
+    own = me["pa"] // 4
+    pa_groups = [own, own + 1 - 2 * lax.rem(own, 2), lax.rem(own + 2, 4), 3 - own]
+
     class Exchange:
         def __init__(self, number, axis, source, target):
             self.number, self.axis, self.source, self.target = number, axis, source, target
@@ -128,7 +132,11 @@
 
         def peer(self, turn, b):
             mine = me[self.axis]
-            return 4 * lax.rem(mine // 4 + turn, 4) + lax.rem(lax.rem(mine, 4) + b, 4)
+            if self.axis == "pa":
+                group = pa_groups[turn]
+            else:
+                group = lax.rem(mine // 4 + turn, 4)
+            return 4 * group + lax.rem(lax.rem(mine, 4) + b, 4)
 
         def send_group(self, turn, own):
             if own:
@@ -275,8 +283,8 @@
                             rhs[last, row : row + 16, column : column + 128] = z_all[
                                 h, 4 * j + 2 * u + v, z
                             ]
-            for to in (1, 2, 3, 0):
-                i = lax.rem(me["pa"] // 4 + to, 4)
+            for turn in (3, 2, 1, 0):
+                i = pa_groups[turn]
                 value = sum(
                     dot_nt(
                         cas[block(i, 256), block(j, 256)], rhs[last, :, 256 * t : 256 * (t + 1)]
@@ -287,7 +295,7 @@
                     value = (value + part_i[block(i, 256), :]).astype(HALF)
                     for b in range(4):
                         i_out[h, 4 * i + b] = value[64 * b : 64 * (b + 1), :]
-                    ex_i[h].send_group(to, to == 0)
+                    ex_i[h].send_group(turn, turn == 0)
                 else:
                     part_i[block(i, 256), :] = value
 
@@ -297,7 +305,7 @@
         for step, turns in enumerate(steps):
             for turn in turns:
                 ex_i[h].receive_group(turn)
-            groups = [lax.rem(me["pa"] // 4 + turn, 4) for turn in turns]
+            groups = [pa_groups[turn] for turn in turns]
             for i in groups:
                 for b in range(4):
                     value = i_all[h, 4 * i + b]
@@ -310,6 +318,8 @@
                 )
                 if h or step:
                     value = value + out_ref[:, columns]
+                if h == PARTS - 1 and step == len(steps) - 1:
+                    value = value * scale
                 out_ref[:, columns] = value
 
     scope = jax.named_scope
@@ -370,29 +380,20 @@
     with scope("x_inverse1"):
         x_inverse(1)
     with scope("y_inverse0"):
-        y_inverse(0, ((0, 1, 3, 2),))
+        y_inverse(0, ((0, 1, 2, 3),))
     with scope("drain_z1"):
         ex_z[1].drain()
         ex_i[0].drain()
     with scope("y_inverse1"):
-        y_inverse(1, ((0, 1), (3,), (2,)))
+        y_inverse(1, ((0, 1), (2,), (3,)))
     with scope("drain"):
         ex_i[1].drain()
 
 
-def finish(scale, total, out_hbm, held, sem):
-    rows = held.shape[0] // 4
-    writes = [
-        pltpu.make_async_copy(
-            held.at[pl.ds(rows * i, rows)], out_hbm.at[pl.ds(rows * i, rows)], sem.at[i]
-        )
-        for i in range(4)
-    ]
-    for i, write in enumerate(writes):
-        held[rows * i : rows * (i + 1), :] = total[rows * i : rows * (i + 1), :] * scale
-        write.start()
-    for write in writes:
-        write.wait()
+def finish(total, out_hbm, sem):
+    write = pltpu.make_async_copy(total, out_hbm, sem)
+    write.start()
+    write.wait()
 
 
 def solution(mesh):
@@ -406,7 +407,7 @@
         anywhere = pl.BlockSpec(memory_space=pl.ANY)
         near = pl.BlockSpec(memory_space=pltpu.VMEM)
         potential = pl.pallas_call(
-            kernel,
+            lambda *refs: kernel(scale, *refs),
             out_shape=jax.ShapeDtypeStruct((256, 1024), jnp.float32),
             in_specs=[anywhere, anywhere, anywhere],
             out_specs=near,
@@ -444,14 +445,11 @@
             name="poisson",
         )(*[pltpu.with_memory_space_constraint(x, pltpu.HBM) for x in (density.reshape(256, 1024), green, cas)])
         potential = pl.pallas_call(
-            lambda *refs: finish(scale, *refs),
+            finish,
             out_shape=jax.ShapeDtypeStruct((256, 1024), jnp.float32),
             in_specs=[near],
             out_specs=anywhere,
-            scratch_shapes=[
-                vmem(256, 1024, dtype=jnp.float32),
-                pltpu.SemaphoreType.DMA((4,)),
-            ],
+            scratch_shapes=[pltpu.SemaphoreType.DMA(())],
             compiler_params=pltpu.CompilerParams(vmem_limit_bytes=8 * 1024 * 1024),
             name="finish",
         )(potential)

time: 69.5 us -> 68.9 us (level)
  no operation moved by 1% of the time
where the time goes in v4:
time: 68.9 us
  Pallas kernels  68.9 us (100%)
    pallas_call x1, Pallas kernels, local(): pl.pallas_call(lambda *refs: kernel(scale, *refs), out_shape=jax.ShapeDty...  67.9 us

profile of v4, /device:TPU:1, one launch (start us, length us, event | category | flops | bytes accessed | tf_op | source)
XLA Modules:
  0.0 68.9 jit_solution(16450537609912379402)
XLA Ops:
  0.0 67.9 %poisson.1.total = f32[256,1024]{1,0:T(8,128)S(1)} custom-call(bf16[256,1024]{1,0:T(8,128)(2,1)} %bitcast.2, f32[8,64,1024]{2,1,0:T(8,128)} %refs_1_.1, bf16[1024,1024]{1,0:T(8,128)(2,1)} %constant.2.clone.refs_2_), custom_call_target="tpu_custom_call" | custom-call | tf_op jit(solution)/shard_map/poisson/pallas_call | solution.py:409
  67.9 1.0 %finish.1 = f32[256,1024]{1,0:T(8,128)} custom-call(f32[256,1024]{1,0:T(8,128)S(1)} %poisson.1.total), custom_call_target="tpu_custom_call" | custom-call | tf_op jit(solution)/shard_map/finish/pallas_call | solution.py:447

commit v5 on v4

--- a/solution.py
+++ b/solution.py
@@ -256,8 +256,8 @@
                     part = part * value[64 * i : 64 * i + 64, 128 * v : 128 * (v + 1)]
                     z_mid[block(4 * j + i, 64), 128 * v : 128 * (v + 1)] = part.astype(HALF)
 
-        @pl.loop(0, 2)
-        def _(j):
+        for near in range(2):
+            j = lax.rem(me["gz"] // 8 + 1 - near, 2)
             value = dot(kron_i[block(j, 256), :], z_mid[...])
             for b in range(8):
                 part = value[32 * b : 32 * b + 32]
@@ -266,8 +266,10 @@
                 )
                 z_out[h, 8 * j + b] = part.astype(HALF)
 
-        ex_z[h].send()
-        ex_z[h].keep()
+            if near:
+                ex_z[h].keep()
+            for b in range(near, 8):
+                ex_z[h].copy(8 * j + lax.rem(lax.rem(me["gz"], 8) + b, 8)).start()
 
     def x_inverse(h):
         for last, turns in enumerate(((2, 1), (3, 0))):

time: 68.9 us -> 68.4 us (level)
  Pallas kernels: 68.9 us -> 68 us
    pallas_call x1, Pallas kernels: 67.9 us -> 67 us  [local(): pl.pallas_call(lambda *refs: kernel(scale, *refs), out_shape=jax.ShapeDty...]
where the time goes in v5:
time: 68.4 us; the launch traced here: 68 us
  Pallas kernels  68 us (99%)
    pallas_call x1, Pallas kernels, local(): pl.pallas_call(lambda *refs: kernel(scale, *refs), out_shape=jax.ShapeDty...  67 us

profile of v5, /device:TPU:1, one launch (start us, length us, event | category | flops | bytes accessed | tf_op | source)
XLA Modules:
  0.0 68.0 jit_solution(9006571814419188787)
XLA Ops:
  0.0 67.0 %poisson.1.total = f32[256,1024]{1,0:T(8,128)S(1)} custom-call(bf16[256,1024]{1,0:T(8,128)(2,1)} %bitcast.2, f32[8,64,1024]{2,1,0:T(8,128)} %refs_1_.1, bf16[1024,1024]{1,0:T(8,128)(2,1)} %constant.2.clone.refs_2_), custom_call_target="tpu_custom_call" | custom-call | tf_op jit(solution)/shard_map/poisson/pallas_call | solution.py:411
  67.0 1.0 %finish.1 = f32[256,1024]{1,0:T(8,128)} custom-call(f32[256,1024]{1,0:T(8,128)S(1)} %poisson.1.total), custom_call_target="tpu_custom_call" | custom-call | tf_op jit(solution)/shard_map/finish/pallas_call | solution.py:449
